TPU v7x, 512 devices: a whole 4x8x8 slice. The times are simulated.
512 devices in a mesh: unit: 2 (over y_1), row: 16 (over y_0, x, core), col: 16 (over z, y_2).
Axes of the slice: x: 4, y: 8 (y_0: 2, y_1: 2, y_2: 2; y = y_0 * 4 + y_1 * 2 + y_2), z: 8, core: 2. Of those that a mesh axis runs over, the one named last changes fastest.
Arguments:
- tracer: float32 [4, 128, 256, 256], P('unit', None, 'row', 'col'), parts along dimension 0, may hold values from -6 to 6
- symbol_x: float32 [128], replicated, may hold values from 0.3 to 3
- symbol_y: float32 [256], replicated, may hold values from 0.3 to 3
- symbol_z: float32 [256], replicated, may hold values from 0.3 to 3
Outputs:
- smoothed: float32 [4, 128, 256, 256], P('unit', None, 'row', 'col'), parts along dimension 0
There are 2 independent parts, one for each index of `unit`. A program takes and returns all parts, laid end to end along the dimension named above; an argument that names none is the same for every part. Nothing has to cross between parts.
All inputs are finite; a program needn't handle non-finite values.
Results may differ from a plain program's by a relative error of at most 0.0003.
Values sent between devices are 32-bit elements.
No kernel may reach another device: no remote copies, remote signals or barrier semaphores. Data moves between devices by JAX's collectives and lax.ppermute only.
A program may use at most 64 MiB of HBM per device.

v0:
```python
import jax
import jax.numpy as jnp
from jax import lax
from jax.sharding import PartitionSpec as P


def mode_table(count):
    rank = jnp.arange(count)
    angle = (
        jnp.pi
        / (4 * count)
        * ((2 * rank[:, None] + 1) * (2 * rank[None, :] + 1) % (8 * count)).astype(jnp.float32)
    )
    return jnp.cos(angle) * (2.0 / count) ** 0.5


def to_modes(values, dim):
    moved = jnp.tensordot(
        values, mode_table(values.shape[dim]), axes=([dim], [0]), precision=lax.Precision.HIGHEST
    )
    return jnp.moveaxis(moved, -1, dim)


def shards(tracer, symbol_x, symbol_y, symbol_z):

    def forward_part(part_values):
        part_values = to_modes(part_values, 1)
        part_values = lax.all_to_all(part_values, "row", split_axis=1, concat_axis=2, tiled=True)
        part_values = to_modes(part_values, 2)
        part_values = lax.all_to_all(part_values, "col", split_axis=2, concat_axis=3, tiled=True)
        return to_modes(part_values, 3)

    def backward_part(part_values):
        part_values = to_modes(part_values, 3)
        part_values = lax.all_to_all(part_values, "col", split_axis=3, concat_axis=2, tiled=True)
        part_values = to_modes(part_values, 2)
        part_values = lax.all_to_all(part_values, "row", split_axis=2, concat_axis=1, tiled=True)
        return to_modes(part_values, 1)

    block_values = forward_part(tracer)
    share_x = block_values.shape[1]
    part_x = lax.dynamic_slice_in_dim(symbol_x, lax.axis_index("row") * share_x, share_x)
    share_y = block_values.shape[2]
    part_y = lax.dynamic_slice_in_dim(symbol_y, lax.axis_index("col") * share_y, share_y)
    symbol = part_x[:, None, None] + part_y[None, :, None] + symbol_z[None, None, :]
    block_values = block_values * lax.rsqrt(symbol)
    block_values = backward_part(block_values)
    return block_values


def solution(mesh):
    in_specs = (P("unit", None, "row", "col"), P(), P(), P())
    out_specs = P("unit", None, "row", "col")
    return jax.shard_map(shards, mesh=mesh, in_specs=in_specs, out_specs=out_specs, check_vma=False)
```

profile of v0, /device:TPU:8, one launch (start us, length us, event | category | flops | bytes accessed | tf_op | source)
XLA Modules:
  0.0 125.6 jit_solution(17801068232473638482)
XLA Ops:
  1.6 1.8 %copy.14 = f32[2,128,16,16]{3,2,0,1:T(8,128)S(1)} copy(f32[2,128,16,16]{1,3,2,0:T(8,128)S(1)} %bitcast.75) | data formatting | bytes 524288 | tf_op jit(solution)/shard_map/transpose | solution.py:21
  3.5 1.5 %reshape.67 = f32[16,1,4096]{2,1,0:T(1,128)} reshape(f32[128,2,16,16]{3,2,1,0:T(8,128)S(1)} %bitcast.64) | data formatting | bytes 524288
  4.9 8.8 %all-to-all-start = ((f32[16,1,4096]{2,1,0:T(1,128)}), f32[16,1,4096]{2,1,0:T(1,128)S(1)}, u32[]{:S(2)}, u32[]{:S(2)}) async-start(f32[16,1,4096]{2,1,0:T(1,128)} %reshape.67), calls=%async_computation | async-start | bytes 524288 | tf_op jit(solution)/shard_map/all_to_all | solution.py:28
  13.7 15.1 %all-to-all-done = f32[16,1,4096]{2,1,0:T(1,128)S(1)} async-done(((f32[16,1,4096]{2,1,0:T(1,128)}), f32[16,1,4096]{2,1,0:T(1,128)S(1)}, u32[]{:S(2)}, u32[]{:S(2)}) %all-to-all-start) | async-done | bytes 262176 | tf_op jit(solution)/shard_map/all_to_all | solution.py:28
  31.3 2.0 %copy.16 = f32[2,8,16,16,16]{3,2,4,1,0:T(8,128)} copy(f32[2,8,16,16,16]{4,3,0,1,2:T(8,128)S(1)} %bitcast.69) | data formatting | bytes 524288 | tf_op jit(solution)/shard_map/all_to_all | solution.py:28
  33.4 2.4 %all_to_all.55 = f32[2,8,256,16]{2,3,1,0:T(8,128)S(1)} reshape(f32[2,8,16,16,16]{3,2,4,1,0:T(8,128)} %copy.16) | data formatting | bytes 524288 | tf_op jit(solution)/shard_map/all_to_all | solution.py:28
  35.8 1.4 %convolution_bitcast_fusion.1 = f32[2,8,256,16]{2,3,1,0:T(8,128)S(1)} fusion(f32[2,8,256,16]{2,3,1,0:T(8,128)S(1)} %all_to_all.55, s32[256]{0:T(256)S(1)} %multiply_add_fusion), kind=kOutput, calls=%fused_computation.6 | convolution fusion | flops 202309632 | bytes 525312 | tf_op jit(solution)/shard_map/dot_general | solution.py:18
  37.3 1.3 %copy.17 = f32[2,8,256,16]{3,1,0,2:T(8,128)S(1)} copy(f32[2,8,256,16]{2,3,1,0:T(8,128)S(1)} %convolution_bitcast_fusion.1) | data formatting | bytes 524288 | tf_op jit(solution)/shard_map/transpose | solution.py:21
  38.6 1.5 %reshape.69 = f32[16,1,4096]{2,1,0:T(1,128)} reshape(f32[256,2,8,16]{3,2,1,0:T(8,128)S(1)} %bitcast.65) | data formatting | bytes 524288
  40.0 11.8 %all-to-all-start.1 = ((f32[16,1,4096]{2,1,0:T(1,128)}), f32[16,1,4096]{2,1,0:T(1,128)S(1)}, u32[]{:S(2)}, u32[]{:S(2)}) async-start(f32[16,1,4096]{2,1,0:T(1,128)} %reshape.69), calls=%async_computation.1 | async-start | bytes 524288 | tf_op jit(solution)/shard_map/all_to_all | solution.py:30
  52.2 10.2 %all-to-all-done.1 = f32[16,1,4096]{2,1,0:T(1,128)S(1)} async-done(((f32[16,1,4096]{2,1,0:T(1,128)}), f32[16,1,4096]{2,1,0:T(1,128)S(1)}, u32[]{:S(2)}, u32[]{:S(2)}) %all-to-all-start.1) | async-done | bytes 262176 | tf_op jit(solution)/shard_map/all_to_all | solution.py:30
  62.4 1.2 reduce.1
  64.3 2.6 %copy.34 = f32[2,8,16,16,16]{4,2,3,1,0:T(8,128)} copy(f32[2,8,16,16,16]{4,1,0,3,2:T(8,128)S(1)} %bitcast.70) | data formatting | bytes 524288 | tf_op jit(solution)/shard_map/all_to_all | solution.py:30
  66.9 2.4 %all_to_all.59 = f32[2,8,16,256]{3,2,1,0:T(8,128)S(1)} reshape(f32[2,8,16,16,16]{4,3,2,1,0:T(8,128)} %bitcast.71) | data formatting | bytes 524288 | tf_op jit(solution)/shard_map/all_to_all | solution.py:30
  69.3 1.4 %convolution_multiply_fusion = f32[2,8,16,256]{3,2,1,0:T(8,128)S(1)} fusion(f32[2,8,16,256]{3,2,1,0:T(8,128)S(1)} %all_to_all.59, f32[8,16,256]{2,1,0:T(8,128)S(1)} %add_rsqrt_fusion, s32[256]{0:T(256)S(1)} %multiply_add_fusion), kind=kOutput, calls=%fused_computation.5 | convolution fusion | flops 202375168 | bytes 656384 | tf_op jit(solution)/shard_map/dot_general | solution.py:18
  70.8 1.4 %fusion.12 = f32[2,8,16,256]{3,2,1,0:T(8,128)S(1)} fusion(f32[2,8,16,256]{3,2,1,0:T(8,128)S(1)} %convolution_multiply_fusion, s32[256]{0:T(256)S(1)} %multiply_add_fusion), kind=kOutput, calls=%fused_computation.19 | convolution fusion | flops 202309632 | bytes 525312 | tf_op jit(solution)/shard_map/dot_general | solution.py:18
  72.2 1.3 %copy.19 = f32[2,8,16,256]{2,1,0,3:T(8,128)S(1)} copy(f32[2,8,16,256]{3,2,1,0:T(8,128)S(1)} %fusion.12) | data formatting | bytes 524288 | tf_op jit(solution)/shard_map/dot_general | solution.py:18
  74.2 14.5 %all_to_all.72 = f32[16,1,4096]{2,1,0:T(1,128)S(1)} all-to-all(f32[16,1,4096]{2,1,0:T(1,128)S(1)} %reshape.71), channel_id=1, replica_groups=mesh['unit'=2,'row'=16,'col'=16] {'col'}, dimensions={0} | all-to-all | bytes 524288 | tf_op jit(solution)/shard_map/all_to_all | solution.py:35
  90.6 2.6 %copy.33 = f32[2,8,16,16,16]{2,3,4,1,0:T(8,128)} copy(f32[2,8,16,16,16]{2,1,0,4,3:T(8,128)S(1)} %bitcast.72) | data formatting | bytes 524288 | tf_op jit(solution)/shard_map/all_to_all | solution.py:35
  93.2 2.4 %all_to_all.63 = f32[2,8,256,16]{2,3,1,0:T(8,128)S(1)} reshape(f32[2,8,16,16,16]{3,2,4,1,0:T(8,128)} %bitcast.73) | data formatting | bytes 524288 | tf_op jit(solution)/shard_map/all_to_all | solution.py:35
  95.7 1.4 %convolution_bitcast_fusion = f32[2,8,256,16]{2,3,1,0:T(8,128)S(1)} fusion(f32[2,8,256,16]{2,3,1,0:T(8,128)S(1)} %all_to_all.63, s32[256]{0:T(256)S(1)} %multiply_add_fusion), kind=kOutput, calls=%fused_computation.4 | convolution fusion | flops 202309632 | bytes 525312 | tf_op jit(solution)/shard_map/dot_general | solution.py:18
  97.1 1.3 %copy.21 = f32[2,8,256,16]{3,1,0,2:T(8,128)S(1)} copy(f32[2,8,256,16]{2,3,1,0:T(8,128)S(1)} %convolution_bitcast_fusion) | data formatting | bytes 524288 | tf_op jit(solution)/shard_map/transpose | solution.py:21
  99.1 19.3 %all_to_all.73 = f32[16,1,4096]{2,1,0:T(1,128)S(1)} all-to-all(f32[16,1,4096]{2,1,0:T(1,128)S(1)} %reshape.73), channel_id=1, replica_groups=mesh['unit'=2,'row'=16,'col'=16] {'row'}, dimensions={0} | all-to-all | bytes 524288 | tf_op jit(solution)/shard_map/all_to_all | solution.py:37
  121.1 4.5 %fusion.2 = f32[2,128,16,16]{1,3,2,0:T(8,128)} fusion(f32[2,128,16,16]{3,2,1,0:T(8,128)S(1)} %bitcast.68, s32[128]{0:T(128)S(1)} %multiply_add_fusion.1), kind=kOutput, calls=%fused_computation.7 | convolution fusion | flops 100909056 | bytes 524800 | tf_op jit(solution)/shard_map/dot_general | solution.py:18
  (26 shorter events, 11.2 us)
Async XLA Ops:
  0.0 1.0 copy-start
  4.9 23.9 %all-to-all-start = ((f32[16,1,4096]{2,1,0:T(1,128)}), f32[16,1,4096]{2,1,0:T(1,128)S(1)}, u32[]{:S(2)}, u32[]{:S(2)}) async-start(f32[16,1,4096]{2,1,0:T(1,128)} %reshape.67), calls=%async_computation | async-start | bytes 524288 | tf_op jit(solution)/shard_map/all_to_all | solution.py:28
  37.3 14.6 %copy-start.2 = (f32[256]{0:T(256)S(1)}, f32[256]{0:T(256)}, u32[]{:S(2)}) copy-start(f32[256]{0:T(256)} %param.6) | copy-start | bytes 3076
  37.3 14.7 %copy-start.3 = (f32[128]{0:T(128)S(1)}, f32[128]{0:T(128)}, u32[]{:S(2)}) copy-start(f32[128]{0:T(128)} %param.5) | copy-start | bytes 1540
  37.3 14.8 %copy-start.1 = (f32[256]{0:T(256)S(1)}, f32[256]{0:T(256)}, u32[]{:S(2)}) copy-start(f32[256]{0:T(256)} %param.7) | copy-start | bytes 3076
  40.0 22.3 %all-to-all-start.1 = ((f32[16,1,4096]{2,1,0:T(1,128)}), f32[16,1,4096]{2,1,0:T(1,128)S(1)}, u32[]{:S(2)}, u32[]{:S(2)}) async-start(f32[16,1,4096]{2,1,0:T(1,128)} %reshape.69), calls=%async_computation.1 | async-start | bytes 524288 | tf_op jit(solution)/shard_map/all_to_all | solution.py:30
where the time goes:
time: 126 us
  blocking collectives  33.8 us (27%)
  local copies, waits for them, and re-layouts  29.7 us (24%)
  waiting for transfers between devices  25.4 us (20%)
  starting transfers between devices  20.6 us (16%)
  matrix products  10.8 us (9%)
  other arithmetic  5.09 us (4%)
    all_to_all x1, blocking collectives, backward_part(): lax.all_to_all(part_values, 'row', split_axis=2, concat_axis=1, tiled=True)  19.3 us
    all_to_all x1, waiting for transfers between devices, forward_part(): lax.all_to_all(part_values, 'row', split_axis=1, concat_axis=2, tiled=True)  15.1 us
    all_to_all x1, blocking collectives, backward_part(): lax.all_to_all(part_values, 'col', split_axis=3, concat_axis=2, tiled=True)  14.5 us
    all_to_all x1, starting transfers between devices, forward_part(): lax.all_to_all(part_values, 'col', split_axis=2, concat_axis=3, tiled=True)  11.8 us
    all_to_all x1, waiting for transfers between devices, forward_part(): lax.all_to_all(part_values, 'col', split_axis=2, concat_axis=3, tiled=True)  10.2 us
    dot_general x5, matrix products, to_modes(): jnp.tensordot(values, mode_table(values.shape[dim]), axes=([dim], [0]), p...  10.1 us
    all_to_all x1, starting transfers between devices, forward_part(): lax.all_to_all(part_values, 'row', split_axis=1, concat_axis=2, tiled=True)  8.77 us
    unnamed x16, local copies, waits for them, and re-layouts  8.21 us
  transfers between devices with their start and end apart: 2, of which 2 were waited for; matrix products, arithmetic and copies ran while one was open for 0% of the time, Pallas kernels for 0%

commit v1 on v0

v1 whole, which is shorter than its diff:
```python
import functools

import jax
import jax.numpy as jnp
import numpy as np
from jax import lax
from jax.experimental import pallas as pl
from jax.experimental.pallas import tpu as pltpu
from jax.sharding import PartitionSpec as P

LANES = 128
BLOCKS = 16
ROWS = 32


def mode_table(count):
    rank = np.arange(count)
    odd = (2 * rank[:, None] + 1) * (2 * rank[None, :] + 1) % (8 * count)
    return np.sqrt(2.0 / count) * np.cos(np.pi / (4 * count) * odd)


def halves(table):
    table = table.astype(np.float32)
    high = table.astype(jnp.bfloat16)
    low = (table - high.astype(np.float32)).astype(jnp.bfloat16)
    return np.stack([high, low])


def split(values):
    high = values.astype(jnp.bfloat16)
    return high, (values - high.astype(jnp.float32)).astype(jnp.bfloat16)


def dot(a, b):
    return jnp.dot(a, b, preferred_element_type=jnp.float32)


def times_table(values, table):
    high, low = split(values)
    return dot(high, table[0]) + (dot(low, table[0]) + dot(high, table[1]))


def table_times(table, values):
    high, low = split(values)
    return dot(table[0], high) + (dot(table[0], low) + dot(table[1], high))


def swap_bits(blocks, pairs):
    lane = lax.broadcasted_iota(jnp.int32, blocks[0].shape, 1)
    for block_bit, lane_bit in pairs:
        mask = (lane & lane_bit) == 0
        blocks = list(blocks)
        for i in range(len(blocks)):
            if i & block_bit:
                continue
            a, b = blocks[i], blocks[i | block_bit]
            blocks[i] = jnp.where(mask, a, pltpu.roll(b, lane_bit, 1))
            blocks[i | block_bit] = jnp.where(mask, pltpu.roll(a, LANES - lane_bit, 1), b)
    return blocks


X_SWAPS = ((1, 1), (2, 2), (4, 4), (8, 8))
Z_SWAPS = ((1, 16), (2, 32), (4, 64))


def x_first(a_ref, table_ref, o_ref):
    table = table_ref[...]
    blocks = [a_ref[pl.ds(k, ROWS, stride=BLOCKS), :] for k in range(BLOCKS)]
    values = times_table(jnp.concatenate(blocks, axis=0), table)
    blocks = [values[k * ROWS : (k + 1) * ROWS] for k in range(BLOCKS)]
    for k, block in enumerate(swap_bits(blocks, X_SWAPS)):
        o_ref[k] = block


def x_last(a_ref, table_ref, o_ref):
    table = table_ref[...]
    blocks = swap_bits([a_ref[k] for k in range(BLOCKS)], X_SWAPS)
    values = times_table(jnp.concatenate(blocks, axis=0), table)
    for k in range(BLOCKS):
        o_ref[pl.ds(k, ROWS, stride=BLOCKS), :] = values[k * ROWS : (k + 1) * ROWS]


def y_middle(a_ref, table_ref, o_ref):
    table = table_ref[...]
    half = ROWS // 2
    planes = [
        jnp.concatenate([a_ref[k, f * half : (f + 1) * half, :] for k in range(BLOCKS)], axis=0)
        for f in range(2)
    ]
    values = table_times(table, jnp.concatenate(planes, axis=1))
    for k in range(BLOCKS):
        for f in range(2):
            o_ref[k, f * half : (f + 1) * half, :] = values[
                k * half : (k + 1) * half, f * LANES : (f + 1) * LANES
            ]


def z_scaled(a_ref, table_ref, sx_ref, sy_ref, sz_ref, o_ref):
    table = table_ref[...]
    half = ROWS // 2
    row = lax.broadcasted_iota(jnp.int32, (half, LANES), 0)
    at_x, at_y = lax.axis_index("row") * 8, lax.axis_index("col") * half
    sy = jnp.full((half, LANES), sy_ref[at_y], jnp.float32)
    for k in range(1, half):
        sy = jnp.where(row == k, sy_ref[at_y + k], sy)
    sy = jnp.concatenate([sy, sy], axis=0)
    sxy = jnp.concatenate([sy + sx_ref[at_x + k] for k in range(8)], axis=0)
    symbol = jnp.concatenate([sxy, sxy], axis=1) + sz_ref[...]
    blocks = swap_bits([a_ref[k] for k in range(BLOCKS)], Z_SWAPS)
    values = jnp.concatenate(
        [jnp.concatenate(blocks[:8], axis=0), jnp.concatenate(blocks[8:], axis=0)], axis=1
    )
    values = times_table(values, table) * lax.rsqrt(symbol)
    values = times_table(values, table)
    blocks = [
        values[k * ROWS : (k + 1) * ROWS, h * LANES : (h + 1) * LANES]
        for h in range(2)
        for k in range(8)
    ]
    for k, block in enumerate(swap_bits(blocks, Z_SWAPS)):
        o_ref[k] = block


VMEM = pl.BlockSpec(memory_space=pltpu.VMEM)
SMEM = pl.BlockSpec(memory_space=pltpu.SMEM)
SPLIT = jax.ShapeDtypeStruct((BLOCKS, ROWS, LANES), jnp.float32)
FLAT = jax.ShapeDtypeStruct((BLOCKS * ROWS, LANES), jnp.float32)


def kernel(body, out, *specs):
    return pl.pallas_call(body, out_shape=out, in_specs=specs, out_specs=VMEM, name=body.__name__)


def shards(tracer, symbol_x, symbol_y, symbol_z):
    lane_x = (np.arange(LANES) % 16) * 8 + np.arange(LANES) // 16
    table_x = mode_table(LANES)
    first_x = jnp.asarray(halves(table_x[:, lane_x]))
    last_x = jnp.asarray(halves(table_x[lane_x, :]))
    table = jnp.asarray(halves(mode_table(256)))
    exchange = functools.partial(lax.all_to_all, split_axis=0, concat_axis=0, tiled=True)

    values = tracer.transpose(0, 2, 3, 1).reshape(FLAT.shape)
    values = kernel(x_first, SPLIT, VMEM, VMEM)(values, first_x)
    values = exchange(values, "row")
    values = kernel(y_middle, SPLIT, VMEM, VMEM)(values, table)
    values = exchange(values, "col")
    values = kernel(z_scaled, SPLIT, VMEM, VMEM, SMEM, SMEM, VMEM)(
        values, table, symbol_x, symbol_y, symbol_z.reshape(1, 256)
    )
    values = exchange(values, "col")
    values = kernel(y_middle, SPLIT, VMEM, VMEM)(values, table)
    values = exchange(values, "row")
    values = kernel(x_last, FLAT, VMEM, VMEM)(values, last_x)
    return values.reshape(2, 16, 16, LANES).transpose(0, 3, 1, 2)


def solution(mesh):
    in_specs = (P("unit", None, "row", "col"), P(), P(), P())
    out_specs = P("unit", None, "row", "col")
    return jax.shard_map(shards, mesh=mesh, in_specs=in_specs, out_specs=out_specs, check_vma=False)
```

time: 126 us -> 93.5 us (0.74)
  the two profiles are of different devices: /device:TPU:8 before, /device:TPU:9 now
where the time goes in v1:
time: 93.5 us; the launch traced here: 93 us
  blocking collectives  81.7 us (87%)
  Pallas kernels  11.2 us (12%)
    all_to_all x2, blocking collectives, shards(): values = exchange(values, 'row')  43.8 us
    all_to_all x2, blocking collectives, shards(): values = exchange(values, 'col')  37.9 us
    pallas_call x2, Pallas kernels, shards(): values = kernel(y_middle, SPLIT, VMEM, VMEM)(values, table)  4 us
    pallas_call x1, Pallas kernels, shards(): kernel(z_scaled, SPLIT, VMEM, VMEM, SMEM, SMEM, VMEM)  2.78 us
    pallas_call x1, Pallas kernels, shards(): values = kernel(x_last, FLAT, VMEM, VMEM)(values, last_x)  2.26 us
    pallas_call x1, Pallas kernels, shards(): values = kernel(x_first, SPLIT, VMEM, VMEM)(values, first_x)  2.19 us

profile of v1, /device:TPU:9, one launch (start us, length us, event | category | flops | bytes accessed | tf_op | source)
XLA Modules:
  0.0 93.0 jit_solution(8486271572893991693)
XLA Ops:
  0.0 2.2 %x_first.1 = f32[16,32,128]{2,1,0:T(8,128)} custom-call(f32[512,128]{1,0:T(8,128)} %bitcast.7, bf16[2,128,128]{2,1,0:T(8,128)(2,1)} %constant.6.clone.table_ref), custom_call_target="tpu_custom_call" | custom-call | tf_op jit(solution)/shard_map/x_first/pallas_call | solution.py:143
  2.2 23.8 %all_to_all.20.a_ref = f32[16,32,128]{2,1,0:T(8,128)} all-to-all(f32[16,32,128]{2,1,0:T(8,128)} %x_first.1), channel_id=1, replica_groups=mesh['unit'=2,'row'=16,'col'=16] {'row'}, dimensions={0} | all-to-all | bytes 524288 | tf_op jit(solution)/shard_map/all_to_all | solution.py:144
  26.0 2.0 %y_middle.2 = f32[16,32,128]{2,1,0:T(8,128)} custom-call(f32[16,32,128]{2,1,0:T(8,128)} %all_to_all.20.a_ref, bf16[2,256,256]{2,1,0:T(8,128)(2,1)} %constant.8.clone.table_ref), custom_call_target="tpu_custom_call" | custom-call | tf_op jit(solution)/shard_map/y_middle/pallas_call | solution.py:145
  28.0 22.8 %all_to_all.21.a_ref = f32[16,32,128]{2,1,0:T(8,128)} all-to-all(f32[16,32,128]{2,1,0:T(8,128)} %y_middle.2), channel_id=1, replica_groups=mesh['unit'=2,'row'=16,'col'=16] {'col'}, dimensions={0} | all-to-all | bytes 524288 | tf_op jit(solution)/shard_map/all_to_all | solution.py:146
  50.8 2.8 %z_scaled.1 = f32[16,32,128]{2,1,0:T(8,128)} custom-call(f32[16,32,128]{2,1,0:T(8,128)} %all_to_all.21.a_ref, bf16[2,256,256]{2,1,0:T(8,128)(2,1)} %constant.8.clone.table_ref, f32[128]{0:T(128)} %sx_ref.1, f32[256]{0:T(256)} %sy_ref.1, f32[1,256]{1,0:T(1,128)} %bitcast.8), custom_call_target="tpu_custom_call" | custom-call | tf_op jit(solution)/shard_map/z_scaled/pallas_call | solution.py:147
  53.5 15.1 %all_to_all.22.a_ref = f32[16,32,128]{2,1,0:T(8,128)} all-to-all(f32[16,32,128]{2,1,0:T(8,128)} %z_scaled.1), channel_id=1, replica_groups=mesh['unit'=2,'row'=16,'col'=16] {'col'}, dimensions={0} | all-to-all | bytes 524288 | tf_op jit(solution)/shard_map/all_to_all | solution.py:150
  68.7 2.0 %y_middle.3 = f32[16,32,128]{2,1,0:T(8,128)} custom-call(f32[16,32,128]{2,1,0:T(8,128)} %all_to_all.22.a_ref, bf16[2,256,256]{2,1,0:T(8,128)(2,1)} %constant.8.clone.table_ref), custom_call_target="tpu_custom_call" | custom-call | tf_op jit(solution)/shard_map/y_middle/pallas_call | solution.py:151
  70.7 20.0 %all_to_all.23.a_ref = f32[16,32,128]{2,1,0:T(8,128)} all-to-all(f32[16,32,128]{2,1,0:T(8,128)} %y_middle.3), channel_id=1, replica_groups=mesh['unit'=2,'row'=16,'col'=16] {'row'}, dimensions={0} | all-to-all | bytes 524288 | tf_op jit(solution)/shard_map/all_to_all | solution.py:152
  90.7 2.3 %x_last.1 = f32[512,128]{1,0:T(8,128)} custom-call(f32[16,32,128]{2,1,0:T(8,128)} %all_to_all.23.a_ref, bf16[2,128,128]{2,1,0:T(8,128)(2,1)} %constant.7.clone.table_ref), custom_call_target="tpu_custom_call" | custom-call | tf_op jit(solution)/shard_map/x_last/pallas_call | solution.py:153

commit v2 on v1

v2 whole, which is shorter than its diff:
```python
import functools

import jax
import jax.numpy as jnp
import numpy as np
from jax import lax
from jax.experimental import pallas as pl
from jax.experimental.pallas import tpu as pltpu
from jax.sharding import PartitionSpec as P

LANES = 128
ROWS = 512
LINES = 256


def mode_table(count):
    rank = np.arange(count)
    odd = (2 * rank[:, None] + 1) * (2 * rank[None, :] + 1) % (8 * count)
    return np.sqrt(2.0 / count) * np.cos(np.pi / (4 * count) * odd)


def halves(table):
    table = table.astype(np.float32)
    high = table.astype(jnp.bfloat16)
    low = (table - high.astype(np.float32)).astype(jnp.bfloat16)
    return np.stack([high, low])


def split(values):
    high = values.astype(jnp.bfloat16)
    return high, (values - high.astype(jnp.float32)).astype(jnp.bfloat16)


def dot(a, b):
    return jnp.dot(a, b, preferred_element_type=jnp.float32)


def times_table(values, table):
    high, low = split(values)
    return dot(high, table[0]) + (dot(low, table[0]) + dot(high, table[1]))


def table_times(table, values):
    high, low = split(values)
    return dot(table[0], high) + (dot(table[0], low) + dot(table[1], high))


def swap_bits(blocks, pairs):
    lane = lax.broadcasted_iota(jnp.int32, blocks[0].shape, 1)
    blocks = list(blocks)
    for block_bit, lane_bit in pairs:
        mask = (lane & lane_bit) == 0
        for i in range(len(blocks)):
            if i & block_bit:
                continue
            a, b = blocks[i], blocks[i | block_bit]
            blocks[i] = jnp.where(mask, a, pltpu.roll(b, lane_bit, 1))
            blocks[i | block_bit] = jnp.where(mask, pltpu.roll(a, LANES - lane_bit, 1), b)
    return blocks


SWAPS = ((2, 16), (4, 32), (8, 64))


def x_first(a_ref, table_ref, o_ref):
    columns = [a_ref[k * LANES : (k + 1) * LANES, :].T for k in range(4)]
    values = table_times(table_ref[...], jnp.concatenate(columns, axis=1))
    for k in range(4):
        o_ref[pl.ds((k // 2) * LINES + k % 2, LANES, stride=2), :] = values[
            :, k * LANES : (k + 1) * LANES
        ]


def x_last(a_ref, table_ref, o_ref):
    columns = [
        a_ref[pl.ds((k // 2) * LINES + k % 2, LANES, stride=2), :].T for k in range(4)
    ]
    o_ref[...] = times_table(jnp.concatenate(columns, axis=0), table_ref[...])


def plane(a_ref, in_ref, z_ref, out_ref, sx_ref, sy_ref, sz_ref, o_ref):
    at_x = (lax.axis_index("row") * 16 + lax.axis_index("col")) % LANES
    sy = [
        jnp.broadcast_to(sy_ref[:, k * LANES : (k + 1) * LANES], (LANES, LANES)).T
        for k in range(2)
    ]
    sy = jnp.concatenate(sy, axis=0) + sx_ref[at_x]
    scale = lax.rsqrt(jnp.concatenate([sy, sy], axis=1) + sz_ref[...])

    blocks = swap_bits([a_ref[pl.ds(k, 16, stride=32), :] for k in range(32)], SWAPS)
    order = [h + 2 * (yl + 8 * c) for c in range(2) for h in range(2) for yl in range(8)]
    values = jnp.concatenate(
        [jnp.concatenate([blocks[k] for k in order[c * 16 : c * 16 + 16]], axis=0) for c in range(2)],
        axis=1,
    )
    table = z_ref[...]
    values = table_times(in_ref[...], values)
    values = times_table(values, table) * scale
    values = times_table(values, table)
    values = table_times(out_ref[...], values)
    for n, k in enumerate(order):
        c, p = divmod(n, 16)
        blocks[k] = values[p * 16 : (p + 1) * 16, c * LANES : (c + 1) * LANES]
    for k, block in enumerate(swap_bits(blocks, SWAPS)):
        o_ref[pl.ds(k, 16, stride=32), :] = block


VMEM = pl.BlockSpec(memory_space=pltpu.VMEM)
SMEM = pl.BlockSpec(memory_space=pltpu.SMEM)
FLAT = jax.ShapeDtypeStruct((ROWS, LANES), jnp.float32)


def kernel(body, *specs):
    return pl.pallas_call(body, out_shape=FLAT, in_specs=specs, out_specs=VMEM, name=body.__name__)


def shards(tracer, symbol_x, symbol_y, symbol_z):
    line = (np.arange(LINES) % 16) * 16 + np.arange(LINES) // 16
    table_x = jnp.asarray(halves(mode_table(LANES)))
    table = mode_table(LINES)
    table_in, table_out = jnp.asarray(halves(table[:, line])), jnp.asarray(halves(table[line, :]))
    table = jnp.asarray(halves(table))
    exchange = functools.partial(
        lax.all_to_all, axis_name=("row", "col"), split_axis=0, concat_axis=0, tiled=True
    )

    values = tracer.transpose(0, 2, 3, 1).reshape(FLAT.shape)
    values = kernel(x_first, VMEM, VMEM)(values, table_x)
    values = exchange(values)
    values = kernel(plane, VMEM, VMEM, VMEM, VMEM, SMEM, VMEM, VMEM)(
        values, table_in, table, table_out, symbol_x, symbol_y.reshape(1, 256), symbol_z.reshape(1, 256)
    )
    values = exchange(values)
    values = kernel(x_last, VMEM, VMEM)(values, table_x)
    return values.reshape(2, 16, 16, LANES).transpose(0, 3, 1, 2)


def solution(mesh):
    in_specs = (P("unit", None, "row", "col"), P(), P(), P())
    out_specs = P("unit", None, "row", "col")
    return jax.shard_map(shards, mesh=mesh, in_specs=in_specs, out_specs=out_specs, check_vma=False)
```

time: 93.5 us -> 76.3 us (0.82)
  the two profiles are of different devices: /device:TPU:9 before, /device:TPU:1 now
where the time goes in v2:
time: 76.3 us; the launch traced here: 76 us
  blocking collectives  68.2 us (89%)
  Pallas kernels  7.75 us (10%)
    all_to_all x2, blocking collectives, shards(): values = exchange(values)  68.2 us
    pallas_call x1, Pallas kernels, shards(): kernel(plane, VMEM, VMEM, VMEM, VMEM, SMEM, VMEM, VMEM)  3.75 us
    pallas_call x1, Pallas kernels, shards(): values = kernel(x_first, VMEM, VMEM)(values, table_x)  2.02 us
    pallas_call x1, Pallas kernels, shards(): values = kernel(x_last, VMEM, VMEM)(values, table_x)  1.97 us

profile of v2, /device:TPU:1, one launch (start us, length us, event | category | flops | bytes accessed | tf_op | source)
XLA Modules:
  0.0 76.0 jit_solution(10185831728567477268)
XLA Ops:
  0.0 2.0 %x_first.1 = f32[512,128]{1,0:T(8,128)} custom-call(f32[512,128]{1,0:T(8,128)} %bitcast.16, bf16[2,128,128]{2,1,0:T(8,128)(2,1)} %constant.8.clone.table_ref), custom_call_target="tpu_custom_call" | custom-call | tf_op jit(solution)/shard_map/x_first/pallas_call | solution.py:128
  2.0 40.2 %all_to_all.22 = f32[256,2,128]{2,1,0:T(2,128)} all-to-all(f32[256,2,128]{2,1,0:T(2,128)} %bitcast.15), channel_id=1, replica_groups=mesh['unit'=2,'row'=16,'col'=16] {'row','col'}, dimensions={0} | all-to-all | bytes 524288 | tf_op jit(solution)/shard_map/all_to_all | solution.py:129
  42.3 3.8 %plane.1 = f32[512,128]{1,0:T(8,128)} custom-call(f32[512,128]{1,0:T(8,128)} %bitcast.12, bf16[2,256,256]{2,1,0:T(8,128)(2,1)} %constant.9.clone.in_ref, bf16[2,256,256]{2,1,0:T(8,128)(2,1)} %constant.11.clone.z_ref, bf16[2,256,256]{2,1,0:T(8,128)(2,1)} %constant.10.clone.out_ref, f32[128]{0:T(128)} %sx_ref.1, f32[1,256]{1,0:T(1,128)} %bitcast.17, ...), custom_call_target="tpu_custom_call" | custom-call | tf_op jit(solution)/shard_map/plane/pallas_call | solution.py:130
  46.0 28.0 %all_to_all.23 = f32[256,2,128]{2,1,0:T(2,128)} all-to-all(f32[256,2,128]{2,1,0:T(2,128)} %bitcast.13), channel_id=1, replica_groups=mesh['unit'=2,'row'=16,'col'=16] {'row','col'}, dimensions={0} | all-to-all | bytes 524288 | tf_op jit(solution)/shard_map/all_to_all | solution.py:133
  74.0 2.0 %x_last.1 = f32[512,128]{1,0:T(8,128)} custom-call(f32[512,128]{1,0:T(8,128)} %bitcast.14, bf16[2,128,128]{2,1,0:T(8,128)(2,1)} %constant.8.clone.table_ref), custom_call_target="tpu_custom_call" | custom-call | tf_op jit(solution)/shard_map/x_last/pallas_call | solution.py:134

commit v3 on v2

--- a/solution.py
+++ b/solution.py
@@ -11,6 +11,10 @@
 LANES = 128
 ROWS = 512
 LINES = 256
+NEAR = ("x", "core")
+FAR = ("y0", "z", "y2")
+NEARS = 8
+FARS = 32
 
 
 def mode_table(count):
@@ -78,8 +82,24 @@
     o_ref[...] = times_table(jnp.concatenate(columns, axis=0), table_ref[...])
 
 
+def to_far(a_ref, o_ref):
+    for near in range(NEARS):
+        for h in range(2):
+            o_ref[pl.ds(near * 2 + h, FARS, stride=2 * NEARS), :] = a_ref[
+                pl.ds(near * 2 * FARS + h, FARS, stride=2), :
+            ]
+
+
+def to_near(a_ref, o_ref):
+    for near in range(NEARS):
+        for h in range(2):
+            o_ref[pl.ds(near * 2 * FARS + h, FARS, stride=2), :] = a_ref[
+                pl.ds(near * 2 + h, FARS, stride=2 * NEARS), :
+            ]
+
+
 def plane(a_ref, in_ref, z_ref, out_ref, sx_ref, sy_ref, sz_ref, o_ref):
-    at_x = (lax.axis_index("row") * 16 + lax.axis_index("col")) % LANES
+    at_x = (lax.axis_index(NEAR) * FARS + lax.axis_index(FAR)) % LANES
     sy = [
         jnp.broadcast_to(sy_ref[:, k * LANES : (k + 1) * LANES], (LANES, LANES)).T
         for k in range(2)
@@ -87,7 +107,12 @@
     sy = jnp.concatenate(sy, axis=0) + sx_ref[at_x]
     scale = lax.rsqrt(jnp.concatenate([sy, sy], axis=1) + sz_ref[...])
 
-    blocks = swap_bits([a_ref[pl.ds(k, 16, stride=32), :] for k in range(32)], SWAPS)
+    starts = [(k // 2) * 16 + k % 2 for k in range(32)]
+    blocks = [
+        jnp.concatenate([a_ref[pl.ds(s + y0 * LINES, 8, stride=2), :] for y0 in range(2)], axis=0)
+        for s in starts
+    ]
+    blocks = swap_bits(blocks, SWAPS)
     order = [h + 2 * (yl + 8 * c) for c in range(2) for h in range(2) for yl in range(8)]
     values = jnp.concatenate(
         [jnp.concatenate([blocks[k] for k in order[c * 16 : c * 16 + 16]], axis=0) for c in range(2)],
@@ -101,8 +126,9 @@
     for n, k in enumerate(order):
         c, p = divmod(n, 16)
         blocks[k] = values[p * 16 : (p + 1) * 16, c * LANES : (c + 1) * LANES]
-    for k, block in enumerate(swap_bits(blocks, SWAPS)):
-        o_ref[pl.ds(k, 16, stride=32), :] = block
+    for s, block in zip(starts, swap_bits(blocks, SWAPS)):
+        for y0 in range(2):
+            o_ref[pl.ds(s + y0 * LINES, 8, stride=2), :] = block[y0 * 8 : y0 * 8 + 8]
 
 
 VMEM = pl.BlockSpec(memory_space=pltpu.VMEM)
@@ -120,22 +146,27 @@
     table = mode_table(LINES)
     table_in, table_out = jnp.asarray(halves(table[:, line])), jnp.asarray(halves(table[line, :]))
     table = jnp.asarray(halves(table))
-    exchange = functools.partial(
-        lax.all_to_all, axis_name=("row", "col"), split_axis=0, concat_axis=0, tiled=True
-    )
+    exchange = functools.partial(lax.all_to_all, split_axis=0, concat_axis=0, tiled=True)
 
     values = tracer.transpose(0, 2, 3, 1).reshape(FLAT.shape)
     values = kernel(x_first, VMEM, VMEM)(values, table_x)
-    values = exchange(values)
+    values = exchange(values, NEAR)
+    values = kernel(to_far, VMEM)(values)
+    values = exchange(values, FAR)
     values = kernel(plane, VMEM, VMEM, VMEM, VMEM, SMEM, VMEM, VMEM)(
         values, table_in, table, table_out, symbol_x, symbol_y.reshape(1, 256), symbol_z.reshape(1, 256)
     )
-    values = exchange(values)
+    values = exchange(values, FAR)
+    values = kernel(to_near, VMEM)(values)
+    values = exchange(values, NEAR)
     values = kernel(x_last, VMEM, VMEM)(values, table_x)
     return values.reshape(2, 16, 16, LANES).transpose(0, 3, 1, 2)
 
 
 def solution(mesh):
-    in_specs = (P("unit", None, "row", "col"), P(), P(), P())
-    out_specs = P("unit", None, "row", "col")
-    return jax.shard_map(shards, mesh=mesh, in_specs=in_specs, out_specs=out_specs, check_vma=False)
+    axes = ("unit", "y0", "x", "core", "z", "y2")
+    mesh = jax.sharding.Mesh(mesh.devices.reshape(2, 2, 4, 2, 8, 2), axes)
+    spec = P("unit", None, ("y0", "x", "core"), ("z", "y2"))
+    return jax.shard_map(
+        shards, mesh=mesh, in_specs=(spec, P(), P(), P()), out_specs=spec, check_vma=False
+    )

time: 76.3 us -> 84.9 us (1.11)
  blocking collectives: 68.2 us -> 73.3 us
  Pallas kernels: 7.75 us -> 11 us
    all_to_all x2 -> x4, blocking collectives: 68.2 us -> 73.3 us  [the longest x2 41.7 us: shards(): values = exchange(values, FAR)]
    pallas_call x0 -> x2, Pallas kernels: none -> 3.5 us  [the longest x1 1.76 us: shards(): values = kernel(to_far, VMEM)(values)]
where the time goes in v3:
time: 84.9 us; the launch traced here: 84.4 us
  blocking collectives  73.3 us (86%)
  Pallas kernels  11 us (13%)
    all_to_all x2, blocking collectives, shards(): values = exchange(values, FAR)  41.7 us
    all_to_all x2, blocking collectives, shards(): values = exchange(values, NEAR)  31.6 us
    pallas_call x1, Pallas kernels, shards(): kernel(plane, VMEM, VMEM, VMEM, VMEM, SMEM, VMEM, VMEM)  3.53 us
    pallas_call x1, Pallas kernels, shards(): values = kernel(x_first, VMEM, VMEM)(values, table_x)  2.02 us
    pallas_call x1, Pallas kernels, shards(): values = kernel(x_last, VMEM, VMEM)(values, table_x)  1.98 us
    pallas_call x1, Pallas kernels, shards(): values = kernel(to_far, VMEM)(values)  1.76 us
    pallas_call x1, Pallas kernels, shards(): values = kernel(to_near, VMEM)(values)  1.74 us

profile of v3, /device:TPU:1, one launch (start us, length us, event | category | flops | bytes accessed | tf_op | source)
XLA Modules:
  0.0 84.4 jit_solution(6076130130044038008)
XLA Ops:
  0.0 2.0 %x_first.1 = f32[512,128]{1,0:T(8,128)} custom-call(f32[512,128]{1,0:T(8,128)} %bitcast.24, bf16[2,128,128]{2,1,0:T(8,128)(2,1)} %constant.8.clone.table_ref), custom_call_target="tpu_custom_call" | custom-call | tf_op jit(solution)/shard_map/x_first/pallas_call | solution.py:152
  2.0 17.3 %all_to_all.44 = f32[8,64,128]{2,1,0:T(8,128)} all-to-all(f32[8,64,128]{2,1,0:T(8,128)} %bitcast.23), channel_id=1, replica_groups=mesh['unit'=2,'y0'=2,'x'=4,'core'=2,'z'=8,'y2'=2] {'x','core'}, dimensions={0} | all-to-all | bytes 524288 | tf_op jit(solution)/shard_map/all_to_all | solution.py:153
  19.4 1.8 %to_far.1 = f32[512,128]{1,0:T(8,128)} custom-call(f32[512,128]{1,0:T(8,128)} %bitcast.19), custom_call_target="tpu_custom_call" | custom-call | tf_op jit(solution)/shard_map/to_far/pallas_call | solution.py:154
  21.1 24.9 %all_to_all.45 = f32[32,16,128]{2,1,0:T(8,128)} all-to-all(f32[32,16,128]{2,1,0:T(8,128)} %bitcast.20), channel_id=1, replica_groups=mesh['unit'=2,'y0'=2,'x'=4,'core'=2,'z'=8,'y2'=2] {'y0','z','y2'}, dimensions={0} | all-to-all | bytes 524288 | tf_op jit(solution)/shard_map/all_to_all | solution.py:155
  46.0 3.5 %plane.1 = f32[512,128]{1,0:T(8,128)} custom-call(f32[512,128]{1,0:T(8,128)} %bitcast.16, bf16[2,256,256]{2,1,0:T(8,128)(2,1)} %constant.9.clone.in_ref, bf16[2,256,256]{2,1,0:T(8,128)(2,1)} %constant.11.clone.z_ref, bf16[2,256,256]{2,1,0:T(8,128)(2,1)} %constant.10.clone.out_ref, f32[128]{0:T(128)} %sx_ref.1, f32[1,256]{1,0:T(1,128)} %bitcast.25, ...), custom_call_target="tpu_custom_call" | custom-call | tf_op jit(solution)/shard_map/plane/pallas_call | solution.py:156
  49.6 16.8 %all_to_all.46 = f32[32,16,128]{2,1,0:T(8,128)} all-to-all(f32[32,16,128]{2,1,0:T(8,128)} %bitcast.17), channel_id=1, replica_groups=mesh['unit'=2,'y0'=2,'x'=4,'core'=2,'z'=8,'y2'=2] {'y0','z','y2'}, dimensions={0} | all-to-all | bytes 524288 | tf_op jit(solution)/shard_map/all_to_all | solution.py:159
  66.4 1.7 %to_near.1 = f32[512,128]{1,0:T(8,128)} custom-call(f32[512,128]{1,0:T(8,128)} %bitcast.21), custom_call_target="tpu_custom_call" | custom-call | tf_op jit(solution)/shard_map/to_near/pallas_call | solution.py:160
  68.1 14.2 %all_to_all.47 = f32[8,64,128]{2,1,0:T(8,128)} all-to-all(f32[8,64,128]{2,1,0:T(8,128)} %bitcast.22), channel_id=1, replica_groups=mesh['unit'=2,'y0'=2,'x'=4,'core'=2,'z'=8,'y2'=2] {'x','core'}, dimensions={0} | all-to-all | bytes 524288 | tf_op jit(solution)/shard_map/all_to_all | solution.py:161
  82.4 2.0 %x_last.1 = f32[512,128]{1,0:T(8,128)} custom-call(f32[512,128]{1,0:T(8,128)} %bitcast.18, bf16[2,128,128]{2,1,0:T(8,128)(2,1)} %constant.8.clone.table_ref), custom_call_target="tpu_custom_call" | custom-call | tf_op jit(solution)/shard_map/x_last/pallas_call | solution.py:162
